TPU v7x, 32 devices: a whole 2x2x4 slice. The times are simulated.
32 devices in a mesh: row: 8 (over y, x, core), col: 4 (over z).
Axes of the slice: x: 2, y: 2, z: 4, core: 2. Of those that a mesh axis runs over, the one named last changes fastest.
Arguments:
- tangents: float32 [192, 128, 6144], P('row', None, 'col'), may hold values from -6 to 6
- base_flow: float32 [192, 128, 192], P('row', None, 'col'), may hold values from -0.0625 to 0.0625
- mode_mask: int32 [192, 192], P('row', 'col'), may hold values 0 or 1
- decay_rates: float32 [128], replicated, may hold values from 1 to 100
- to_eigen: float32 [128, 128], replicated, may hold values from -0.5 to 0.5
- from_eigen: float32 [128, 128], replicated, may hold values from -0.5 to 0.5
Outputs:
- vectors: float32 [192, 128, 6144], P('row', None, 'col')
- growth: float32 [32], replicated
Inputs may be any that keep to these rules, and one draw needn't show every extreme that they name: `mode_mask`: 1 keeps a mode pair of the linearized product, 0 removes it.
All inputs are finite; a program needn't handle non-finite values. No bound on the sum of `mode_mask` on one device may be relied on, other than what follows from the above.
Results may differ from a plain program's by a relative error of at most 0.00005.
Values sent between devices are 32-bit elements; how exact they have to be, the bound alone decides.
A program may use at most 256 MiB of HBM per device.

v0:
```python
import math
import jax
import jax.numpy as jnp
from jax import lax
from jax.sharding import PartitionSpec as P

PRECISE = lax.Precision.HIGHEST
STEP_COEF = 10.0
VISCOSITY = 0.01
ALPHA_X = 0.5
BETA_Z = 1.0


def local_waves(points_count, first_index, length):
    indices = first_index + jnp.arange(length, dtype=jnp.int32)
    middle = points_count // 2
    return jnp.where(indices <= middle, indices, indices - middle).astype(jnp.float32)


def synthesis(points_count):
    points = jnp.arange(points_count, dtype=jnp.int32)[:, None]
    mode_index = jnp.arange(points_count, dtype=jnp.int32)[None, :]
    middle = points_count // 2
    wave_index = jnp.where(mode_index <= middle, mode_index, mode_index - middle)
    turn_count = (points * wave_index % points_count).astype(jnp.float32)
    angles = turn_count * (2.0 * math.pi / points_count)
    return jnp.where(mode_index <= middle, jnp.cos(angles), jnp.sin(angles))


def analysis(points_count):
    mode_index = jnp.arange(points_count, dtype=jnp.int32)
    middle = points_count // 2
    weights = jnp.where(
        (mode_index == 0) | (mode_index == middle),
        jnp.float32(1.0 / points_count),
        jnp.float32(2.0 / points_count),
    )
    return weights[:, None] * synthesis(points_count).T


def derivative_analysis(points_count, wave_scale):
    rows_index = jnp.arange(points_count, dtype=jnp.int32)[:, None]
    cols_index = jnp.arange(points_count, dtype=jnp.int32)[None, :]
    middle = points_count // 2
    rising = (cols_index == rows_index + middle) & (rows_index >= 1) & (rows_index < middle)
    falling = (rows_index == cols_index + middle) & (cols_index >= 1) & (cols_index < middle)
    rows_float = jnp.broadcast_to(rows_index.astype(jnp.float32), (points_count, points_count))
    cols_float = jnp.broadcast_to(cols_index.astype(jnp.float32), (points_count, points_count))
    derivative = jnp.where(rising, rows_float, jnp.float32(0.0)) - jnp.where(
        falling, cols_float, jnp.float32(0.0)
    )
    return -wave_scale * jnp.dot(derivative, analysis(points_count), precision=PRECISE)


def denominators(decay_rates, x_count, z_count, x_start, z_start, x_length, z_length):
    wave_x = ALPHA_X * local_waves(x_count, x_start, x_length)
    wave_z = BETA_Z * local_waves(z_count, z_start, z_length)
    return (
        STEP_COEF
        + VISCOSITY * (wave_x[:, None, None] ** 2 + wave_z[None, None, :] ** 2)
        + decay_rates[None, :, None]
    )


def body(tangents, base_flow, mode_mask, decay_rates, to_eigen, from_eigen):
    x_length, y_count, zv_length = tangents.shape
    z_length = base_flow.shape[2]
    vec_count = zv_length // z_length
    row_devices = lax.axis_size("row")
    col_devices = lax.axis_size("col")
    x_count = x_length * row_devices
    z_count = z_length * col_devices
    x_synthesis = synthesis(x_count)
    z_synthesis = synthesis(z_count)
    x_derivative = derivative_analysis(x_count, ALPHA_X)
    z_analysis = analysis(z_count)
    all_devices = row_devices * col_devices
    plane_count = y_count // all_devices
    stacked = tangents.reshape(x_length, y_count, 1, zv_length)
    speed_stack = base_flow.reshape(x_length, y_count, 1, z_length)
    planes, speed_field = (
        lax.all_to_all(stacked, ("row", "col"), split_axis=1, concat_axis=2, tiled=True),
        lax.all_to_all(speed_stack, ("row", "col"), split_axis=1, concat_axis=2, tiled=True),
    )
    x_table = x_synthesis.reshape(x_count, row_devices, x_length)
    z_table = z_synthesis.reshape(z_count, col_devices, z_length)
    planes = planes.reshape(x_length, plane_count, row_devices, col_devices, z_length, vec_count)
    physical = jnp.einsum("myrcnv,prm->ypcnv", planes, x_table, precision=PRECISE)
    physical = jnp.einsum("ypcnv,scn->ypsv", physical, z_table, precision=PRECISE)
    speed_field = speed_field.reshape(x_length, plane_count, row_devices, col_devices, z_length)
    speed_field = jnp.einsum("myrcn,prm->ypcn", speed_field, x_table, precision=PRECISE)
    speed_field = jnp.einsum("ypcn,scn->yps", speed_field, z_table, precision=PRECISE)
    product = physical * speed_field[:, :, :, None]
    returned = jnp.einsum("ypsv,ns->ypnv", product, z_analysis, precision=PRECISE)
    returned = jnp.einsum("ypnv,mp->ymnv", returned, x_derivative, precision=PRECISE)
    returned = returned.reshape(
        plane_count, row_devices, x_length, col_devices, z_length, vec_count
    )
    returned = jnp.transpose(returned, (2, 0, 1, 3, 4, 5)).reshape(
        x_length, plane_count, all_devices, zv_length
    )
    nonlinear = lax.all_to_all(returned, ("row", "col"), split_axis=2, concat_axis=1, tiled=True)
    nonlinear = nonlinear.reshape(x_length, y_count, zv_length)
    x_start = lax.axis_index("row") * x_length
    z_start = lax.axis_index("col") * z_length
    divisor = denominators(decay_rates, x_count, z_count, x_start, z_start, x_length, z_length)
    retained = mode_mask.astype(jnp.float32)[:, None, :, None]
    nonlinear = nonlinear.reshape(x_length, y_count, z_length, vec_count) * retained
    right_side = STEP_COEF * tangents.reshape(x_length, y_count, z_length, vec_count) + nonlinear
    eigen_part = jnp.einsum(
        "ji,mic->mjc", to_eigen, right_side.reshape(x_length, y_count, zv_length), precision=PRECISE
    )
    eigen_part = eigen_part.reshape(x_length, y_count, z_length, vec_count) / divisor[:, :, :, None]
    stepped = jnp.einsum(
        "yj,mjc->myc",
        from_eigen,
        eigen_part.reshape(x_length, y_count, zv_length),
        precision=PRECISE,
    )
    columns = stepped.reshape(x_length * y_count * z_length, vec_count)
    cell_count = x_count * y_count * z_count
    identity = jnp.eye(vec_count, dtype=jnp.float32)

    def refine(block):
        local_gram = jnp.einsum("cv,cu->vu", block, block, precision=PRECISE)
        gram_matrix = lax.psum(local_gram, ("row", "col")) / cell_count
        lower_factor = jnp.linalg.cholesky(gram_matrix)
        inverse = jax.scipy.linalg.solve_triangular(lower_factor, identity, lower=True)
        refined = jnp.einsum("cv,uv->cu", block, inverse, precision=PRECISE)
        return (refined, jnp.log(jnp.diagonal(lower_factor)))

    first_pass, first_growth = refine(columns)
    orthonormal, second_growth = refine(first_pass)
    growth = first_growth + second_growth
    return (orthonormal.reshape(x_length, y_count, zv_length), growth)


def solution(mesh):
    placed = (P("row", None, "col"), P("row", None, "col"), P("row", "col"), P(), P(), P())
    return jax.shard_map(
        body, mesh=mesh, in_specs=placed, out_specs=(P("row", None, "col"), P()), check_vma=False
    )
```

profile of v0, /device:TPU:0, one launch (start us, length us, event | category | flops | bytes accessed | tf_op | source)
XLA Modules:
  0.0 2041.6 jit_solution(13407496623339631732)
XLA Ops:
  0.6 0.0 copy-start
  0.6 1.6 copy.62
  2.3 0.1 bitcast_bitcast_fusion
  2.4 2.4 reshape.235
  4.8 7.3 all-to-all-start.1
  12.1 19.6 copy.107
  31.7 0.0 all-to-all-done.1
  31.7 6.1 all-to-all-start
  38.0 1.3 fusion.19
  39.3 0.9 fusion.148
  40.2 0.5 broadcast.375
  40.7 2.0 reduce.4
  42.7 0.7 reshape.236
  43.4 3.4 fusion.16
  46.8 1.7 convolution_bitcast_fusion.1
  48.5 394.0 %all-to-all-done = f32[24,128,1,1536]{3,0,2,1:T(8,128)} async-done(((f32[24,128,1,1536]{3,0,2,1:T(8,128)}), f32[24,128,1,1536]{3,0,2,1:T(8,128)}, u32[]{:S(2)}, u32[]{:S(2)}) %all-to-all-start) | async-done | bytes 18874400 | tf_op jit(solution)/shard_map/all_to_all | solution.py:82
  442.5 19.6 copy.106
  462.2 44.8 %reshape.204 = f32[24,4,8,4,48,32]{5,4,3,2,1,0:T(8,128)} reshape(f32[24,4,32,1,1536]{4,2,1,0,3:T(8,128)} %bitcast.144) | data formatting | bytes 37748736 | tf_op jit(solution)/shard_map/reshape | solution.py:87
  507.0 67.4 %copy.60 = f32[24,4,8,4,48,32]{4,0,2,5,3,1:T(8,128)} copy(f32[24,4,8,4,48,32]{5,4,3,2,1,0:T(8,128)} %reshape.204) | data formatting | bytes 37748736 | tf_op jit(solution)/shard_map/reshape | solution.py:87
  574.4 86.3 %fusion.28 = f32[192,4,4,48,32,1]{0,3,5,4,2,1:T(8,128)} fusion(f32[24,4,8,4,48,32]{4,0,2,5,3,1:T(8,128)} %copy.60, f32[192,8,24,1,1,1]{0,2,1,5,4,3:T(8,128)S(1)} %fusion.148), kind=kOutput, calls=%fused_computation.36 | convolution fusion | flops 10871635968 | bytes 37896192 | tf_op jit(solution)/shard_map/myrcnv,prm->ypcnv/dot_general | solution.py:88
  660.7 31.7 %fusion.1 = f32[192,4,192,32,1]{2,0,3,4,1:T(8,128)} fusion(f32[192,4,4,48,32,1]{0,3,5,4,2,1:T(8,128)} %fusion.28, s32[4,48]{1,0:T(4,128)S(1)} %add_select_fusion.4, pred[4,48]{1,0:T(4,128)(4,1)S(1)} %fusion.103), kind=kOutput, calls=%fused_computation.4 | convolution fusion | flops 10872004608 | bytes 37749696 | tf_op jit(solution)/shard_map/ypcnv,scn->ypsv/dot_general | solution.py:89
  692.4 30.9 %fusion = f32[192,4,192,32]{2,0,3,1:T(8,128)} fusion(f32[192,4,192,32,1]{2,0,3,4,1:T(8,128)} %fusion.1, f32[4,192,192]{1,2,0:T(8,128)S(1)} %convolution_bitcast_fusion.1, s32[192]{0:T(256)S(1)} %get-tuple-element.8, f32[192]{0:T(256)S(1)} %or_select_fusion, pred[192]{0:T(512)(128)(4,1)S(1)} %get-tuple-element.10), kind=kOutput, calls=%fused_computation.3 | convolution fusion | flops 10876760064 | bytes 38340288 | tf_op jit(solution)/shard_map/ypsv,ns->ypnv/dot_general | solution.py:94
  723.3 28.1 %fusion.9 = f32[4,192,192,32]{2,1,3,0:T(8,128)} fusion(f32[192,192,1,1]{1,0,3,2:T(8,128)S(1)} %fusion.19, f32[192,4,192,32]{2,0,3,1:T(8,128)} %fusion), kind=kOutput, calls=%fused_computation.16 | convolution fusion | flops 10871635968 | bytes 37896192 | tf_op jit(solution)/shard_map/ypnv,mp->ymnv/dot_general | solution.py:95
  751.4 44.9 %reshape.207 = f32[4,8,24,4,48,32]{4,3,2,1,5,0:T(4,128)} reshape(f32[4,192,192,32]{2,1,3,0:T(8,128)} %fusion.9) | data formatting | bytes 37748736 | tf_op jit(solution)/shard_map/reshape | solution.py:96
  796.3 71.3 %copy.68 = f32[4,8,24,4,48,32]{5,4,3,1,0,2:T(8,128)} copy(f32[4,8,24,4,48,32]{4,3,2,1,5,0:T(4,128)} %reshape.207) | data formatting | bytes 37748736 | tf_op jit(solution)/shard_map/reshape | solution.py:96
  867.7 53.6 %reshape.208 = f32[24,4,32,1536]{3,2,1,0:T(8,128)} reshape(f32[24,4,8,4,48,32]{5,4,3,2,1,0:T(8,128)} %bitcast.33) | data formatting | bytes 37748736 | tf_op jit(solution)/shard_map/reshape | solution.py:99
  921.3 23.2 %copy.69 = f32[24,4,32,1536]{3,1,0,2:T(4,128)} copy(f32[24,4,32,1536]{3,2,1,0:T(8,128)} %reshape.208) | data formatting | bytes 37748736 | tf_op jit(solution)/shard_map/reshape | solution.py:99
  944.5 17.9 all-to-all-start.2
  962.4 0.0 copy-done.4
  962.5 0.2 mul.165
  962.7 0.3 mul.166
  962.9 0.5 or_bitcast_fusion
  963.5 0.1 multiply_add_fusion
  963.5 0.2 broadcast_add_fusion
  963.8 403.4 %all-to-all-done.2 = f32[24,4,32,1536]{3,1,0,2:T(4,128)} async-done(((f32[24,4,32,1536]{3,1,0,2:T(4,128)}), f32[24,4,32,1536]{3,1,0,2:T(4,128)}, u32[]{:S(2)}, u32[]{:S(2)}) %all-to-all-start.2) | async-done | bytes 18874400 | tf_op jit(solution)/shard_map/all_to_all | solution.py:102
  1367.1 12.1 copy.70
  1379.2 20.4 %fusion.5 = f32[24,128,1536]{2,0,1:T(8,128)} fusion(f32[24,4,32,1536]{3,0,1,2:T(8,128)S(1)} %copy.70, f32[24,128,1536]{2,1,0:T(8,128)} %param.9, f32[24,1536]{1,0:T(8,128)S(1)} %mul.166), kind=kLoop, calls=%fused_computation.9 | loop fusion | flops 14155776 | bytes 56770560 | tf_op jit(solution)/shard_map/add | solution.py:109
  1399.7 38.5 %bitcast_divide_fusion = f32[24,128,1536]{1,2,0:T(8,128)S(1)} fusion(f32[24,128,48]{1,2,0:T(8,128)S(1)} %broadcast_add_fusion, f32[24,128,1536]{2,0,1:T(8,128)} %fusion.5, f32[128,128]{1,0:T(8,128)S(1)} %copy-done), kind=kOutput, calls=%fused_computation.10 | convolution fusion | flops 7252475904 | bytes 38404096 | tf_op jit(solution)/shard_map/ji,mic->mjc/dot_general | solution.py:110
  1438.2 0.0 copy-done.3
  1438.2 17.9 convolution_bitcast_fusion
  1456.1 18.7 copy.72
  1474.8 44.8 %reshape.209 = f32[147456,32]{1,0:T(8,128)} reshape(f32[24,128,1536]{2,1,0:T(8,128)} %copy.72) | data formatting | bytes 37748736 | tf_op jit(solution)/shard_map/reshape | solution.py:120
  1519.6 129.6 %fusion.129 = f32[32,32]{0,1:T(8,128)S(1)} fusion(f32[147456,32]{1,0:T(8,128)} %reshape.209), kind=kOutput, calls=%fused_computation.172 | convolution fusion | flops 1811939328 | bytes 18878464 | tf_op jit(solution)/shard_map/cv,cu->vu/dot_general | solution.py:125
  1649.2 53.2 %psum.14 = f32[32,32]{0,1:T(8,128)S(1)} all-reduce(f32[32,32]{0,1:T(8,128)S(1)} %fusion.129), channel_id=1, replica_groups=mesh['row'=8,'col'=4] {'row','col'}, use_global_device_ids=true, to_apply=%region_0.1 | all-reduce | flops 1024 | bytes 8192 | tf_op jit(solution)/shard_map/psum | solution.py:126
  1702.4 0.1 copy.74
  1702.5 2.9 cholesky.44
  1705.5 0.6 compare_reduce_fusion.1
  1706.1 0.7 select_bitcast_fusion.1
  1706.8 2.4 custom-call.10
  1709.2 0.2 fusion.95
  1709.4 85.6 %fusion.130 = f32[147456,32]{0,1:T(8,128)} fusion(f32[147456,32]{1,0:T(8,128)} %reshape.209, f32[32,32]{1,0:T(8,128)S(1)} %fusion.95), kind=kOutput, calls=%fused_computation.173 | convolution fusion | flops 1811939328 | bytes 37752832 | tf_op jit(solution)/shard_map/cv,uv->cu/dot_general | solution.py:129
  1795.0 19.3 fusion.131
  1814.4 39.5 %psum.15 = f32[32,32]{0,1:T(8,128)S(1)} all-reduce(f32[32,32]{0,1:T(8,128)S(1)} %fusion.131), channel_id=1, replica_groups=mesh['row'=8,'col'=4] {'row','col'}, use_global_device_ids=true, to_apply=%region_3.6 | all-reduce | flops 1024 | bytes 8192 | tf_op jit(solution)/shard_map/psum | solution.py:126
  1853.9 0.1 copy.76
  1854.0 2.9 cholesky.55
  1856.9 0.6 compare_reduce_fusion
  1857.6 0.7 select_bitcast_fusion
  1858.2 0.7 gather_fusion.1
  1859.0 0.7 gather_fusion
  1859.7 2.4 custom-call.11
  1862.1 0.2 fusion.93
  1862.3 124.7 %fusion.132 = f32[147456,32]{1,0:T(8,128)} fusion(f32[147456,32]{0,1:T(8,128)} %fusion.130, f32[32,32]{1,0:T(8,128)S(1)} %fusion.93), kind=kOutput, calls=%fused_computation.175 | convolution fusion | flops 1811939328 | bytes 37752832 | tf_op jit(solution)/shard_map/cv,uv->cu/dot_general | solution.py:129
  1987.1 53.6 %reshape.210 = f32[24,128,1536]{2,1,0:T(8,128)} reshape(f32[147456,32]{1,0:T(8,128)} %fusion.132) | data formatting | bytes 37748736 | tf_op jit(solution)/shard_map/reshape | solution.py:135
  2040.7 0.5 log_add_fusion
  (27 shorter events, 0.2 us)
Async XLA Ops:
  0.6 1399.0 %copy-start = (f32[128,128]{1,0:T(8,128)S(1)}, f32[128,128]{1,0:T(8,128)}, u32[]{:S(2)}) copy-start(f32[128,128]{1,0:T(8,128)} %param.13) | copy-start | bytes 196612
  4.8 27.0 %all-to-all-start.1 = ((f32[32,1,4608]{2,1,0:T(1,128)}), f32[32,1,4608]{2,1,0:T(1,128)S(1)}, u32[]{:S(2)}, u32[]{:S(2)}) async-start(f32[32,1,4608]{2,1,0:T(1,128)} %reshape.235), calls=%async_computation.1 | async-start | bytes 1179648 | tf_op jit(solution)/shard_map/all_to_all | solution.py:83
  31.7 410.8 %all-to-all-start = ((f32[24,128,1,1536]{3,0,2,1:T(8,128)}), f32[24,128,1,1536]{3,0,2,1:T(8,128)}, u32[]{:S(2)}, u32[]{:S(2)}) async-start(f32[24,128,1,1536]{3,0,2,1:T(8,128)} %bitcast.143), calls=%async_computation | async-start | bytes 37748736 | tf_op jit(solution)/shard_map/all_to_all | solution.py:82
  944.5 17.9 copy-start.4
  944.5 19.0 copy-start.5
  944.5 422.6 %all-to-all-start.2 = ((f32[24,4,32,1536]{3,1,0,2:T(4,128)}), f32[24,4,32,1536]{3,1,0,2:T(4,128)}, u32[]{:S(2)}, u32[]{:S(2)}) async-start(f32[24,4,32,1536]{3,1,0,2:T(4,128)} %copy.69), calls=%async_computation.2 | async-start | bytes 37748736 | tf_op jit(solution)/shard_map/all_to_all | solution.py:102
  1399.7 38.5 %copy-start.3 = (f32[128,128]{1,0:T(8,128)S(1)}, f32[128,128]{1,0:T(8,128)}, u32[]{:S(2)}) copy-start(f32[128,128]{1,0:T(8,128)} %param.14) | copy-start | bytes 196612
  1795.0 63.2 %copy-start.2 = (s32[32]{0:T(128)S(1)}, s32[32]{0:T(128)}, u32[]{:S(2)}) copy-start(s32[32]{0:T(128)} %or_bitcast_fusion) | copy-start | bytes 388
  1987.1 54.1 %copy-start.1 = (f32[128,128]{1,0:T(8,128)S(1)}, f32[128,128]{1,0:T(8,128)}, u32[]{:S(2)}) copy-start(f32[128,128]{1,0:T(8,128)} %param.13) | copy-start | bytes 196612
where the time goes:
time: 2060 us; the launch traced here: 2040 us
  waiting for transfers between devices  797 us (39%)
  matrix products  600 us (29%)
  local copies, waits for them, and re-layouts  481 us (23%)
  blocking collectives  92.7 us (4%)
  other arithmetic  38.1 us (2%)
  starting transfers between devices  31.4 us (2%)
    all_to_all x1, waiting for transfers between devices, body(): lax.all_to_all(returned, ('row', 'col'), split_axis=2, concat_axis=1, til...  403 us
    all_to_all x1, waiting for transfers between devices, body(): lax.all_to_all(stacked, ('row', 'col'), split_axis=1, concat_axis=2, tile...  394 us
    dot_general x2, matrix products, refine(): refined = jnp.einsum('cv,uv->cu', block, inverse, precision=PRECISE)  210 us
    dot_general x2, matrix products, refine(): local_gram = jnp.einsum('cv,cu->vu', block, block, precision=PRECISE)  149 us
    reshape x2, local copies, waits for them, and re-layouts, body(): returned.reshape(plane_count, row_devices, x_length, col_devices, z_lengt...  116 us
    reshape x2, local copies, waits for them, and re-layouts, body(): planes.reshape(x_length, plane_count, row_devices, col_devices, z_length,...  112 us
    psum x2, blocking collectives, refine(): gram_matrix = lax.psum(local_gram, ('row', 'col')) / cell_count  92.7 us
    dot_general x1, matrix products, body(): jnp.einsum('myrcnv,prm->ypcnv', planes, x_table, precision=PRECISE)  86.3 us
  transfers between devices with their start and end apart: 3, of which 2 were waited for; matrix products, arithmetic and copies ran while one was open for 2% of the time, Pallas kernels for 0%

commit v1 on v0

--- a/solution.py
+++ b/solution.py
@@ -99,7 +99,15 @@
     returned = jnp.transpose(returned, (2, 0, 1, 3, 4, 5)).reshape(
         x_length, plane_count, all_devices, zv_length
     )
-    nonlinear = lax.all_to_all(returned, ("row", "col"), split_axis=2, concat_axis=1, tiled=True)
+    nonlinear = jnp.concatenate(
+        lax.all_to_all(
+            jnp.stack(jnp.split(returned, lax.axis_size(("row", "col")), axis=2)),
+            ("row", "col"),
+            0,
+            0,
+        ),
+        axis=1,
+    )
     nonlinear = nonlinear.reshape(x_length, y_count, zv_length)
     x_start = lax.axis_index("row") * x_length
     z_start = lax.axis_index("col") * z_length

time: 2060 us -> 2160 us (1.049)
  local copies, waits for them, and re-layouts: 481 us -> 578 us
    unnamed x17 -> x48, local copies, waits for them, and re-layouts: 24.4 us -> 140 us
    reshape x2 -> x1, local copies, waits for them, and re-layouts: 76.8 us -> 53.8 us  [body(): jnp.transpose(returned, (2, 0, 1, 3, 4, 5))]
  transfers between devices with their start and end apart: 3 -> 3, of which waited for: 2 -> 2; matrix products, arithmetic and copies ran while one was open for 2% -> 1% of each run, Pallas kernels for 0% -> 0%
where the time goes in v1:
time: 2160 us; the launch traced here: 2150 us
  waiting for transfers between devices  797 us (37%)
  matrix products  611 us (28%)
  local copies, waits for them, and re-layouts  578 us (27%)
  blocking collectives  92.7 us (4%)
  other arithmetic  38.1 us (2%)
  starting transfers between devices  31.1 us (1%)
    all_to_all x1, waiting for transfers between devices, body(): lax.all_to_all(jnp.stack(jnp.split(returned, lax.axis_size(('row', 'col')...  403 us
    all_to_all x1, waiting for transfers between devices, body(): lax.all_to_all(stacked, ('row', 'col'), split_axis=1, concat_axis=2, tile...  394 us
    dot_general x2, matrix products, refine(): refined = jnp.einsum('cv,uv->cu', block, inverse, precision=PRECISE)  210 us
    dot_general x2, matrix products, refine(): local_gram = jnp.einsum('cv,cu->vu', block, block, precision=PRECISE)  149 us
    unnamed x48, local copies, waits for them, and re-layouts  140 us
    reshape x2, local copies, waits for them, and re-layouts, body(): returned.reshape(plane_count, row_devices, x_length, col_devices, z_lengt...  116 us
    reshape x2, local copies, waits for them, and re-layouts, body(): planes.reshape(x_length, plane_count, row_devices, col_devices, z_length,...  112 us
    dot_general x1, matrix products, body(): jnp.einsum('myrcnv,prm->ypcnv', planes, x_table, precision=PRECISE)  97.4 us
  transfers between devices with their start and end apart: 3, of which 2 were waited for; matrix products, arithmetic and copies ran while one was open for 1% of the time, Pallas kernels for 0%

profile of v1, /device:TPU:0, one launch (start us, length us, event | category | flops | bytes accessed | tf_op | source)
XLA Modules:
  0.0 2149.0 jit_solution(6921346409612188401)
XLA Ops:
  4.8 7.3 all-to-all-start.1
  12.1 19.6 copy.137
  31.7 6.2 all-to-all-start
  43.5 3.4 fusion.16
  48.6 394.0 %all-to-all-done = f32[24,128,1,1536]{3,0,2,1:T(8,128)} async-done(((f32[24,128,1,1536]{3,0,2,1:T(8,128)}), f32[24,128,1,1536]{3,0,2,1:T(8,128)}, u32[]{:S(2)}, u32[]{:S(2)}) %all-to-all-start) | async-done | bytes 18874400 | tf_op jit(solution)/shard_map/all_to_all | solution.py:82
  442.6 19.6 copy.136
  462.2 44.8 %reshape.206 = f32[24,4,8,4,48,32]{5,4,3,2,1,0:T(8,128)} reshape(f32[24,4,32,1,1536]{4,2,1,0,3:T(8,128)} %bitcast.269) | data formatting | bytes 37748736 | tf_op jit(solution)/shard_map/reshape | solution.py:87
  507.1 67.4 %copy.91 = f32[24,4,8,4,48,32]{4,0,2,5,3,1:T(8,128)} copy(f32[24,4,8,4,48,32]{5,4,3,2,1,0:T(8,128)} %reshape.206) | data formatting | bytes 37748736 | tf_op jit(solution)/shard_map/reshape | solution.py:87
  574.5 97.4 %fusion.60 = f32[192,4,4,48,32,1]{0,3,5,4,2,1:T(8,128)} fusion(f32[24,4,8,4,48,32]{4,0,2,5,3,1:T(8,128)} %copy.91, f32[192,8,24,1,1,1]{0,2,1,5,4,3:T(8,128)S(1)} %fusion.180), kind=kOutput, calls=%fused_computation.100 | convolution fusion | flops 10871635968 | bytes 37896192 | tf_op jit(solution)/shard_map/myrcnv,prm->ypcnv/dot_general | solution.py:88
  671.9 31.7 %fusion.1 = f32[192,4,192,32,1]{2,0,3,4,1:T(8,128)} fusion(f32[192,4,4,48,32,1]{0,3,5,4,2,1:T(8,128)} %fusion.60, s32[4,48]{1,0:T(4,128)S(1)} %add_select_fusion.4, pred[4,48]{1,0:T(4,128)(4,1)S(1)} %fusion.135), kind=kOutput, calls=%fused_computation.4 | convolution fusion | flops 10872004608 | bytes 37749696 | tf_op jit(solution)/shard_map/ypcnv,scn->ypsv/dot_general | solution.py:89
  703.6 30.9 %fusion = f32[192,4,192,32]{2,0,3,1:T(8,128)} fusion(f32[192,4,192,32,1]{2,0,3,4,1:T(8,128)} %fusion.1, f32[4,192,192]{1,2,0:T(8,128)S(1)} %convolution_bitcast_fusion.1, s32[192]{0:T(256)S(1)} %get-tuple-element.8, f32[192]{0:T(256)S(1)} %or_select_fusion, pred[192]{0:T(512)(128)(4,1)S(1)} %get-tuple-element.10), kind=kOutput, calls=%fused_computation.3 | convolution fusion | flops 10876760064 | bytes 38340288 | tf_op jit(solution)/shard_map/ypsv,ns->ypnv/dot_general | solution.py:94
  734.5 28.1 %fusion.9 = f32[4,192,192,32]{2,1,3,0:T(8,128)} fusion(f32[192,192,1,1]{1,0,3,2:T(8,128)S(1)} %fusion.19, f32[192,4,192,32]{2,0,3,1:T(8,128)} %fusion), kind=kOutput, calls=%fused_computation.16 | convolution fusion | flops 10871635968 | bytes 37896192 | tf_op jit(solution)/shard_map/ypnv,mp->ymnv/dot_general | solution.py:95
  762.5 44.9 %reshape.209 = f32[4,8,24,4,48,32]{4,3,2,1,5,0:T(4,128)} reshape(f32[4,192,192,32]{2,1,3,0:T(8,128)} %fusion.9) | data formatting | bytes 37748736 | tf_op jit(solution)/shard_map/reshape | solution.py:96
  807.5 71.3 %copy.99 = f32[4,8,24,4,48,32]{5,4,3,1,0,2:T(8,128)} copy(f32[4,8,24,4,48,32]{4,3,2,1,5,0:T(4,128)} %reshape.209) | data formatting | bytes 37748736 | tf_op jit(solution)/shard_map/reshape | solution.py:96
  878.8 53.8 %reshape.210 = f32[24,4,32,1536]{3,2,1,0:T(8,128)} reshape(f32[24,4,8,4,48,32]{5,4,3,2,1,0:T(8,128)} %bitcast.33) | data formatting | bytes 37748736 | tf_op jit(solution)/shard_map/reshape | solution.py:99
  932.6 3.5 fusion.51
  936.1 3.8 fusion.50
  939.9 3.8 fusion.49
  943.6 3.7 fusion.48
  947.4 3.7 fusion.47
  951.1 3.7 fusion.46
  954.9 3.7 fusion.45
  958.6 3.8 fusion.44
  962.4 3.5 fusion.43
  965.9 3.7 fusion.42
  969.6 3.8 fusion.41
  973.4 3.8 fusion.40
  977.2 3.8 fusion.39
  981.0 3.7 fusion.38
  984.7 3.8 fusion.37
  988.5 3.8 fusion.36
  992.2 3.5 fusion.35
  995.7 3.8 fusion.34
  999.5 3.8 fusion.33
  1003.3 3.8 fusion.32
  1007.0 4.2 fusion.31
  1011.3 3.8 fusion.30
  1015.0 3.7 fusion.29
  1018.8 3.7 fusion.28
  1022.5 3.5 fusion.27
  1026.0 3.8 fusion.26
  1029.8 3.8 fusion.25
  1033.5 3.8 fusion.24
  1037.3 3.7 fusion.23
  1041.0 3.8 fusion.22
  1044.8 3.7 fusion.21
  1048.5 3.8 fusion.20
  1052.3 17.5 all-to-all-start.2
  1071.2 403.4 %all-to-all-done.2 = f32[32,24,4,1,1536]{4,3,2,1,0:T(1,128)} async-done(((f32[32,24,4,1,1536]{4,3,2,1,0:T(1,128)}), f32[32,24,4,1,1536]{4,3,2,1,0:T(1,128)}, u32[]{:S(2)}, u32[]{:S(2)}) %all-to-all-start.2) | async-done | bytes 18874400 | tf_op jit(solution)/shard_map/all_to_all | solution.py:103
  1474.5 12.1 copy.100
  1486.7 20.4 fusion.5
  1507.1 38.5 %bitcast_divide_fusion = f32[24,128,1536]{1,2,0:T(8,128)S(1)} fusion(f32[24,128,48]{1,2,0:T(8,128)S(1)} %broadcast_add_fusion, f32[24,128,1536]{2,0,1:T(8,128)} %fusion.5, f32[128,128]{1,0:T(8,128)S(1)} %copy-done), kind=kOutput, calls=%fused_computation.8 | convolution fusion | flops 7252475904 | bytes 38404096 | tf_op jit(solution)/shard_map/ji,mic->mjc/dot_general | solution.py:118
  1545.6 17.9 convolution_bitcast_fusion
  1563.5 18.7 copy.102
  1582.2 44.8 %reshape.212 = f32[147456,32]{1,0:T(8,128)} reshape(f32[24,128,1536]{2,1,0:T(8,128)} %copy.102) | data formatting | bytes 37748736 | tf_op jit(solution)/shard_map/reshape | solution.py:128
  1627.0 129.6 %fusion.161 = f32[32,32]{0,1:T(8,128)S(1)} fusion(f32[147456,32]{1,0:T(8,128)} %reshape.212), kind=kOutput, calls=%fused_computation.236 | convolution fusion | flops 1811939328 | bytes 18878464 | tf_op jit(solution)/shard_map/cv,cu->vu/dot_general | solution.py:133
  1756.7 53.2 %psum.14 = f32[32,32]{0,1:T(8,128)S(1)} all-reduce(f32[32,32]{0,1:T(8,128)S(1)} %fusion.161), channel_id=1, replica_groups=mesh['row'=8,'col'=4] {'row','col'}, use_global_device_ids=true, to_apply=%region_0.1 | all-reduce | flops 1024 | bytes 8192 | tf_op jit(solution)/shard_map/psum | solution.py:134
  1810.0 2.9 cholesky.44
  1816.9 85.6 %fusion.162 = f32[147456,32]{0,1:T(8,128)} fusion(f32[147456,32]{1,0:T(8,128)} %reshape.212, f32[32,32]{1,0:T(8,128)S(1)} %fusion.127), kind=kOutput, calls=%fused_computation.237 | convolution fusion | flops 1811939328 | bytes 37752832 | tf_op jit(solution)/shard_map/cv,uv->cu/dot_general | solution.py:137
  1902.5 19.3 fusion.163
  1921.8 39.5 %psum.15 = f32[32,32]{0,1:T(8,128)S(1)} all-reduce(f32[32,32]{0,1:T(8,128)S(1)} %fusion.163), channel_id=1, replica_groups=mesh['row'=8,'col'=4] {'row','col'}, use_global_device_ids=true, to_apply=%region_3.6 | all-reduce | flops 1024 | bytes 8192 | tf_op jit(solution)/shard_map/psum | solution.py:134
  1961.4 2.9 cholesky.55
  1969.8 124.7 %fusion.164 = f32[147456,32]{1,0:T(8,128)} fusion(f32[147456,32]{0,1:T(8,128)} %fusion.162, f32[32,32]{1,0:T(8,128)S(1)} %fusion.125), kind=kOutput, calls=%fused_computation.239 | convolution fusion | flops 1811939328 | bytes 37752832 | tf_op jit(solution)/shard_map/cv,uv->cu/dot_general | solution.py:137
  2094.5 53.6 %reshape.213 = f32[24,128,1536]{2,1,0:T(8,128)} reshape(f32[147456,32]{1,0:T(8,128)} %fusion.164) | data formatting | bytes 37748736 | tf_op jit(solution)/shard_map/reshape | solution.py:143
  (58 shorter events, 22.7 us)
Async XLA Ops:
  0.6 1506.5 %copy-start = (f32[128,128]{1,0:T(8,128)S(1)}, f32[128,128]{1,0:T(8,128)}, u32[]{:S(2)}) copy-start(f32[128,128]{1,0:T(8,128)} %param.13) | copy-start | bytes 196612
  4.8 27.0 %all-to-all-start.1 = ((f32[32,1,4608]{2,1,0:T(1,128)}), f32[32,1,4608]{2,1,0:T(1,128)S(1)}, u32[]{:S(2)}, u32[]{:S(2)}) async-start(f32[32,1,4608]{2,1,0:T(1,128)} %reshape.238), calls=%async_computation.1 | async-start | bytes 1179648 | tf_op jit(solution)/shard_map/all_to_all | solution.py:83
  31.7 410.9 %all-to-all-start = ((f32[24,128,1,1536]{3,0,2,1:T(8,128)}), f32[24,128,1,1536]{3,0,2,1:T(8,128)}, u32[]{:S(2)}, u32[]{:S(2)}) async-start(f32[24,128,1,1536]{3,0,2,1:T(8,128)} %bitcast.268), calls=%async_computation | async-start | bytes 37748736 | tf_op jit(solution)/shard_map/all_to_all | solution.py:82
  1052.3 17.5 copy-start.4
  1052.3 18.6 copy-start.5
  1052.3 422.2 %all-to-all-start.2 = ((f32[32,24,4,1,1536]{4,3,2,1,0:T(1,128)}), f32[32,24,4,1,1536]{4,3,2,1,0:T(1,128)}, u32[]{:S(2)}, u32[]{:S(2)}) async-start(f32[32,24,4,1,1536]{4,3,2,1,0:T(1,128)} %fusion.20), calls=%async_computation.2 | async-start | bytes 37748736 | tf_op jit(solution)/shard_map/all_to_all | solution.py:103
  1507.1 38.5 %copy-start.3 = (f32[128,128]{1,0:T(8,128)S(1)}, f32[128,128]{1,0:T(8,128)}, u32[]{:S(2)}) copy-start(f32[128,128]{1,0:T(8,128)} %param.14) | copy-start | bytes 196612
  1902.5 63.2 %copy-start.2 = (s32[32]{0:T(128)S(1)}, s32[32]{0:T(128)}, u32[]{:S(2)}) copy-start(s32[32]{0:T(128)} %or_bitcast_fusion) | copy-start | bytes 388
  2094.5 54.1 %copy-start.1 = (f32[128,128]{1,0:T(8,128)S(1)}, f32[128,128]{1,0:T(8,128)}, u32[]{:S(2)}) copy-start(f32[128,128]{1,0:T(8,128)} %param.13) | copy-start | bytes 196612
